TPU v7x, 32 devices: a 4x2x2 block of a 4x4x8 slice. The times are simulated.
32 devices in a mesh: dp: 4 (over y, z), tp: 8 (over x, core).
Axes of the slice: x: 4, y: 2, z: 2, core: 2. Of those that a mesh axis runs over, the one named last changes fastest.
The devices are a block of a 4x4x8 slice.
Arguments:
- hidden: bfloat16 [128, 1536], P('dp'), parts along dimension 0
- lengths: int32 [128], P('dp'), parts along dimension 0
- choice: int32 [2, 128, 8], P(None, 'dp'), parts along dimension 1
- keys_one: bfloat16 [128, 128, 8, 64], P('dp', 'tp'), parts along dimension 0
- vals_one: bfloat16 [128, 128, 8, 64], P('dp', 'tp'), parts along dimension 0
- keys_two: bfloat16 [128, 128, 8, 64], P('dp', 'tp'), parts along dimension 0
- vals_two: bfloat16 [128, 128, 8, 64], P('dp', 'tp'), parts along dimension 0
- g_attn: bfloat16 [2, 1536], replicated
- w_q: bfloat16 [2, 1536, 1536], P(None, None, 'tp')
- w_k: bfloat16 [2, 1536, 512], P(None, None, 'tp')
- w_v: bfloat16 [2, 1536, 512], P(None, None, 'tp')
- w_o: bfloat16 [2, 1536, 1536], P(None, 'tp')
- g_mlp: bfloat16 [2, 1536], replicated
- w_router: bfloat16 [2, 1536, 40], replicated
- w_gate: bfloat16 [2, 40, 1536, 512], P(None, None, None, 'tp')
- w_up: bfloat16 [2, 40, 1536, 512], P(None, None, None, 'tp')
- w_down: bfloat16 [2, 40, 512, 1536], P(None, None, 'tp')
Outputs:
- output 1: bfloat16 [128, 1536], P('dp'), parts along dimension 0
- output 2: bfloat16 [128, 128, 8, 64], P('dp', None, 'tp'), parts along dimension 0
- output 3: bfloat16 [128, 128, 8, 64], P('dp', None, 'tp'), parts along dimension 0
- output 4: bfloat16 [128, 128, 8, 64], P('dp', None, 'tp'), parts along dimension 0
- output 5: bfloat16 [128, 128, 8, 64], P('dp', None, 'tp'), parts along dimension 0
There are 4 independent parts. A program takes and returns all parts, laid end to end along the dimension named above; an argument that names none is the same for every part.
All inputs are finite; a program needn't handle non-finite values.
Results may differ from a plain program's by a relative error of at most 0.02.
Values are sent between devices in bfloat16 or wider.
A program may use at most 768 MiB of HBM per device.

v0:
```python
import jax
import jax.numpy as jnp
from jax import lax
from jax.sharding import PartitionSpec as P

EPS = 1e-5
THETA = 1000000.0


def rms_norm(tensor, gain_vec):
    tensor_f = tensor.astype(jnp.float32)
    scale = lax.rsqrt(jnp.mean(tensor_f * tensor_f, axis=-1, keepdims=True) + EPS)
    return (tensor_f * scale * gain_vec.astype(jnp.float32)).astype(jnp.bfloat16)


def apply_rope(tensor, lengths):
    head_dim = tensor.shape[-1]
    half_dim = head_dim // 2
    inv_freq = THETA ** (-2.0 * jnp.arange(half_dim, dtype=jnp.float32) / head_dim)
    angle = lengths.astype(jnp.float32)[:, None] * inv_freq[None, :]
    cos_part = jnp.cos(angle)[:, None, :]
    sin_part = jnp.sin(angle)[:, None, :]
    lower_half = tensor[..., :half_dim]
    upper_half = tensor[..., half_dim:]
    return jnp.concatenate([lower_half * cos_part - upper_half * sin_part, upper_half * cos_part + lower_half * sin_part], axis=-1)


def expert_block(x_mid, choice, g_mlp, w_router, w_gate, w_up, w_down):
    normed = rms_norm(x_mid, g_mlp)
    logits = jnp.dot(normed, w_router, preferred_element_type=jnp.float32)
    onehot = (choice[:, :, None] == jnp.arange(w_router.shape[1])[None, None, :]).astype(jnp.float32)
    gate_prob = jax.nn.softmax(jnp.sum(onehot * logits[:, None, :], axis=-1), axis=-1)
    gate_mat = jnp.sum(gate_prob[:, :, None] * onehot, axis=1)
    gate_act = jnp.einsum('bd,edf->bef', normed, w_gate, preferred_element_type=jnp.float32)
    up_act = jnp.einsum('bd,edf->bef', normed, w_up, preferred_element_type=jnp.float32)
    expert_in = (jax.nn.silu(gate_act) * up_act * gate_mat[:, :, None]).astype(jnp.bfloat16)
    return jnp.einsum('bef,efd->bd', expert_in, w_down, preferred_element_type=jnp.float32)


def decode_layer(hidden, lengths, choice, key_cache, val_cache, g_attn, w_q, w_k, w_v, w_o, g_mlp, w_router, w_gate, w_up, w_down):
    batch_rows, seq_len, kv_heads, head_dim = key_cache.shape
    num_heads = w_q.shape[1] // head_dim
    normed = rms_norm(hidden, g_attn)
    query_rot = apply_rope(jnp.dot(normed, w_q, preferred_element_type=jnp.float32).reshape(batch_rows, num_heads, head_dim), lengths).astype(jnp.bfloat16)
    key_new = apply_rope(jnp.dot(normed, w_k, preferred_element_type=jnp.float32).reshape(batch_rows, kv_heads, head_dim), lengths).astype(jnp.bfloat16)
    val_new = jnp.dot(normed, w_v, preferred_element_type=jnp.float32).astype(jnp.bfloat16).reshape(batch_rows, kv_heads, head_dim)
    positions = jnp.arange(seq_len)
    is_new = (positions[None, :] == lengths[:, None])[:, :, None, None]
    key_cache = jnp.where(is_new, key_new[:, None], key_cache)
    val_cache = jnp.where(is_new, val_new[:, None], val_cache)
    query_grp = query_rot.reshape(batch_rows, kv_heads, num_heads // kv_heads, head_dim)
    scores = jnp.einsum('bgrd,bsgd->bgrs', query_grp, key_cache, preferred_element_type=jnp.float32) * head_dim ** -0.5
    is_valid = (positions[None, :] <= lengths[:, None])[:, None, None, :]
    attn_prob = jax.nn.softmax(jnp.where(is_valid, scores, -1e30), axis=-1).astype(jnp.bfloat16)
    attn_vec = jnp.einsum('bgrs,bsgd->bgrd', attn_prob, val_cache, preferred_element_type=jnp.float32).astype(jnp.bfloat16).reshape(batch_rows, num_heads * head_dim)
    attn_sum = lax.psum(jnp.dot(attn_vec, w_o, preferred_element_type=jnp.float32).astype(jnp.bfloat16), 'tp')
    x_mid = (hidden.astype(jnp.float32) + attn_sum.astype(jnp.float32)).astype(jnp.bfloat16)
    moe_sum = lax.psum(expert_block(x_mid, choice, g_mlp, w_router, w_gate, w_up, w_down).astype(jnp.bfloat16), 'tp')
    return (x_mid.astype(jnp.float32) + moe_sum.astype(jnp.float32)).astype(jnp.bfloat16), key_cache, val_cache


def solution(mesh):
    seq_spec = P('dp', 'tp', None, None)
    head_spec = P('dp', None, 'tp', None)
    col_spec = P(None, None, 'tp')
    ff_spec = P(None, None, None, 'tp')

    def local_step(hidden, lengths, choice, keys_one, vals_one, keys_two, vals_two, g_attn, w_q, w_k, w_v, w_o, g_mlp, w_router, w_gate, w_up, w_down):
        moved = [lax.all_to_all(cache_blk, 'tp', 2, 1, tiled=True) for cache_blk in (keys_one, vals_one, keys_two, vals_two)]
        results = []
        for layer_idx in range(2):
            hidden, key_cache, val_cache = decode_layer(hidden, lengths, choice[layer_idx], moved[2 * layer_idx], moved[2 * layer_idx + 1], g_attn[layer_idx], w_q[layer_idx], w_k[layer_idx], w_v[layer_idx], w_o[layer_idx], g_mlp[layer_idx], w_router[layer_idx], w_gate[layer_idx], w_up[layer_idx], w_down[layer_idx])
            results.append(key_cache)
            results.append(val_cache)
        return (hidden, results[0], results[1], results[2], results[3])

    return jax.shard_map(local_step, mesh=mesh, in_specs=(P('dp', None), P('dp'), P(None, 'dp', None), seq_spec, seq_spec, seq_spec, seq_spec, P(), col_spec, col_spec, col_spec, P(None, 'tp', None), P(), P(), ff_spec, ff_spec, P(None, None, 'tp', None)), out_specs=(P('dp', None), head_spec, head_spec, head_spec, head_spec), check_vma=False)
```

profile of v0, /device:TPU:81, one launch (start us, length us, event | category | flops | bytes accessed | tf_op | source)
XLA Modules:
  0.0 337.4 jit_solution(16465931818854490697)
XLA Ops:
  7.2 1.5 copy.152
  8.7 1.5 reshape.468
  10.2 6.1 %all-to-all-start.1 = ((bf16[8,2,16384]{2,1,0:T(2,128)(2,1)}), bf16[8,2,16384]{2,1,0:T(2,128)(2,1)S(1)}, u32[]{:S(2)}, u32[]{:S(2)}) async-start(bf16[8,2,16384]{2,1,0:T(2,128)(2,1)} %reshape.468), calls=%async_computation.1 | async-start | bytes 1048576 | tf_op jit(solution)/shard_map/all_to_all | solution.py:69
  16.4 1.4 copy.150
  17.7 1.5 reshape.466
  19.4 1.4 copy.153
  20.8 1.5 reshape.470
  22.5 1.1 convolution_bitcast_fusion.1
  23.8 0.9 fusion.157
  24.7 0.4 fusion.118
  25.1 1.4 copy.151
  26.5 1.5 reshape.472
  28.3 0.2 convolution_convert_fusion.5
  28.6 4.8 %all-to-all-start = ((bf16[8,2,16384]{2,1,0:T(2,128)(2,1)}), bf16[8,2,16384]{2,1,0:T(2,128)(2,1)S(1)}, u32[]{:S(2)}, u32[]{:S(2)}) async-start(bf16[8,2,16384]{2,1,0:T(2,128)(2,1)} %reshape.470), calls=%async_computation | async-start | bytes 1048576 | tf_op jit(solution)/shard_map/all_to_all | solution.py:69
  33.5 0.7 reshape.469
  34.1 0.2 bitcast_bitcast_fusion.2
  34.3 8.2 %all-to-all-done = bf16[8,2,16384]{2,1,0:T(2,128)(2,1)S(1)} async-done(((bf16[8,2,16384]{2,1,0:T(2,128)(2,1)}), bf16[8,2,16384]{2,1,0:T(2,128)(2,1)S(1)}, u32[]{:S(2)}, u32[]{:S(2)}) %all-to-all-start) | async-done | bytes 524320 | tf_op jit(solution)/shard_map/all_to_all | solution.py:69
  42.5 5.2 %all-to-all-start.3 = ((bf16[8,2,16384]{2,1,0:T(2,128)(2,1)}), bf16[8,2,16384]{2,1,0:T(2,128)(2,1)}, u32[]{:S(2)}, u32[]{:S(2)}) async-start(bf16[8,2,16384]{2,1,0:T(2,128)(2,1)} %reshape.466), calls=%async_computation.3 | async-start | bytes 1048576 | tf_op jit(solution)/shard_map/all_to_all | solution.py:69
  47.8 0.7 reshape.471
  48.6 0.3 copy.105
  48.9 0.9 fusion.55
  49.8 0.3 copy.109
  50.2 0.2 fusion.158
  50.4 1.1 convolution_convert_fusion.3
  51.6 5.5 %all-to-all-done.3 = bf16[8,2,16384]{2,1,0:T(2,128)(2,1)} async-done(((bf16[8,2,16384]{2,1,0:T(2,128)(2,1)}), bf16[8,2,16384]{2,1,0:T(2,128)(2,1)}, u32[]{:S(2)}, u32[]{:S(2)}) %all-to-all-start.3) | async-done | bytes 524320 | tf_op jit(solution)/shard_map/all_to_all | solution.py:69
  57.1 5.1 %all-to-all-start.2 = ((bf16[8,2,16384]{2,1,0:T(2,128)(2,1)}), bf16[8,2,16384]{2,1,0:T(2,128)(2,1)}, u32[]{:S(2)}, u32[]{:S(2)}) async-start(bf16[8,2,16384]{2,1,0:T(2,128)(2,1)} %reshape.472), calls=%async_computation.2 | async-start | bytes 1048576 | tf_op jit(solution)/shard_map/all_to_all | solution.py:69
  62.2 1.9 convolution_convert_fusion.1
  64.2 0.2 all-reduce.7.cloned.1.call-start
  64.5 2.3 reshape.467
  67.0 4.6 %all-to-all-done.2 = bf16[8,2,16384]{2,1,0:T(2,128)(2,1)} async-done(((bf16[8,2,16384]{2,1,0:T(2,128)(2,1)}), bf16[8,2,16384]{2,1,0:T(2,128)(2,1)}, u32[]{:S(2)}, u32[]{:S(2)}) %all-to-all-start.2) | async-done | bytes 524320 | tf_op jit(solution)/shard_map/all_to_all | solution.py:69
  71.5 2.3 reshape.473
  73.8 46.1 %all-reduce.5.cloned.1.call-done = bf16[32,1536]{1,0:T(8,128)(2,1)} async-done(((bf16[32,1536]{1,0:T(8,128)(2,1)}), bf16[32,1536]{1,0:T(8,128)(2,1)}) %all-reduce.5.cloned.1.call-update) | async-done | bytes 98320 | tf_op jit(solution)/shard_map/psum | solution.py:56
  120.0 1.0 fusion.84
  121.0 1.0 fusion.86
  122.0 7.7 %fusion.12 = f32[32,40,64]{2,0,1:T(8,128)} fusion(bf16[2,40,1536,64]{2,3,1,0:T(8,128)(2,1)} %param.31, bf16[32,1536]{1,0:T(8,128)(2,1)S(1)} %fusion.86), kind=kOutput, calls=%fused_computation.12 | convolution fusion | flops 251658240 | bytes 8290304 | tf_op jit(solution)/shard_map/bd,edf->bef/dot_general | solution.py:34
  129.8 1.0 fusion.106
  130.8 0.2 select_reduce_fusion.3
  131.5 9.3 %fusion.29 = bf16[32,1536]{1,0:T(8,128)(2,1)} fusion(bf16[2,40,64,1536]{3,2,1,0:T(8,128)(2,1)} %param.33, bf16[2,40,1536,64]{2,3,1,0:T(8,128)(2,1)} %param.32, f32[32,40,64]{2,0,1:T(8,128)} %fusion.12, f32[32,40]{0,1:T(8,128)S(1)} %copy.115, bf16[32,1536]{1,0:T(8,128)(2,1)S(1)} %fusion.86), kind=kOutput, calls=%fused_computation.23 | convolution fusion | flops 503939072 | bytes 16585728 | tf_op jit(solution)/shard_map/bef,efd->bd/dot_general | solution.py:37
  141.2 0.3 copy.121
  141.4 0.3 copy.117
  141.8 51.8 %all-reduce.7.cloned.1.call-done = bf16[32,1536]{1,0:T(8,128)(2,1)} async-done(((bf16[32,1536]{1,0:T(8,128)(2,1)}), bf16[32,1536]{1,0:T(8,128)(2,1)}) %all-reduce.7.cloned.1.call-update) | async-done | bytes 98320 | tf_op jit(solution)/shard_map/psum | solution.py:58
  193.5 1.0 fusion.88
  194.6 1.2 convolution_convert_fusion.4
  195.7 1.2 convolution_bitcast_fusion
  197.1 1.4 fusion.113
  198.8 0.9 fusion.54
  199.7 0.2 fusion.159
  199.9 1.1 convolution_convert_fusion.2
  201.1 1.9 convolution_convert_fusion
  203.1 0.3 all-reduce.11.cloned.1.call-start
  203.5 52.3 %all-reduce.9.cloned.1.call-done = bf16[32,1536]{1,0:T(8,128)(2,1)} async-done(((bf16[32,1536]{1,0:T(8,128)(2,1)}), bf16[32,1536]{1,0:T(8,128)(2,1)}) %all-reduce.9.cloned.1.call-update) | async-done | bytes 98320 | tf_op jit(solution)/shard_map/psum | solution.py:56
  255.7 1.0 fusion.92
  256.8 1.0 fusion.94
  257.8 7.7 %fusion.6 = f32[32,40,64]{2,0,1:T(8,128)} fusion(bf16[2,40,1536,64]{2,3,1,0:T(8,128)(2,1)} %param.31, bf16[32,1536]{1,0:T(8,128)(2,1)S(1)} %fusion.94), kind=kOutput, calls=%fused_computation.6 | convolution fusion | flops 251658240 | bytes 8290304 | tf_op jit(solution)/shard_map/bd,edf->bef/dot_general | solution.py:34
  265.5 1.0 fusion.104
  266.5 0.2 select_reduce_fusion.1
  267.3 9.3 %fusion.26 = bf16[32,1536]{1,0:T(8,128)(2,1)} fusion(bf16[2,40,64,1536]{3,2,1,0:T(8,128)(2,1)} %param.33, bf16[2,40,1536,64]{2,3,1,0:T(8,128)(2,1)} %param.32, f32[32,40,64]{2,0,1:T(8,128)} %fusion.6, f32[32,40]{0,1:T(8,128)S(1)} %copy.127, bf16[32,1536]{1,0:T(8,128)(2,1)S(1)} %fusion.94), kind=kOutput, calls=%fused_computation.22 | convolution fusion | flops 503939072 | bytes 16585728 | tf_op jit(solution)/shard_map/bef,efd->bd/dot_general | solution.py:37
  276.7 5.1 %bitcast_select_fusion = (bf16[32,128,1,64]{3,1,0,2:T(8,128)(2,1)}, bf16[32,128,1,64]{3,1,0,2:T(8,128)(2,1)}, bf16[32,128,1,64]{3,1,0,2:T(8,128)(2,1)}, bf16[32,128,1,64]{3,1,0,2:T(8,128)(2,1)}) fusion(bf16[32,8,16,1,64]{4,2,1,0,3:T(8,128)(2,1)S(1)} %copy.121, pred[32,128]{1,0:T(8,128)(4,1)S(1)} %get-tuple-element.50, ...), kind=kLoop, calls=%fused_computation.46 | loop fusion | flops 1048576 | bytes 4214784 | tf_op jit(solution)/shard_map/jit(_where)/select_n | solution.py:50
  281.8 2.3 copy.132
  284.2 2.3 copy.133
  286.5 2.3 copy.134
  288.8 2.3 copy.135
  291.2 38.1 %all-reduce.11.cloned.1.call-done = bf16[32,1536]{1,0:T(8,128)(2,1)} async-done(((bf16[32,1536]{1,0:T(8,128)(2,1)}), bf16[32,1536]{1,0:T(8,128)(2,1)}) %all-reduce.11.cloned.1.call-update) | async-done | bytes 98320 | tf_op jit(solution)/shard_map/psum | solution.py:58
  329.3 1.6 fusion.95
  (72 shorter events, 3.6 us)
Async XLA Ops:
  7.2 12.1 %copy-start.7 = (bf16[2,1536]{1,0:T(2,128)(2,1)S(1)}, bf16[2,1536]{1,0:T(2,128)(2,1)}, u32[]{:S(2)}) copy-start(bf16[2,1536]{1,0:T(2,128)(2,1)} %param.24) | copy-start | bytes 18436
  7.2 12.1 %copy-start.3 = (bf16[32,1536]{1,0:T(8,128)(2,1)S(1)}, bf16[32,1536]{1,0:T(8,128)(2,1)}, u32[]{:S(2)}) copy-start(bf16[32,1536]{1,0:T(8,128)(2,1)} %param.17) | copy-start | bytes 294916
  7.2 15.1 %copy-start.10 = (s32[32]{0:T(128)S(1)}, s32[32]{0:T(128)}, u32[]{:S(2)}) copy-start(s32[32]{0:T(128)} %param.18) | copy-start | bytes 388
  7.2 16.6 %copy-start.4 = (bf16[2,1536,192]{1,2,0:T(8,128)(2,1)S(1)}, bf16[2,1536,192]{1,2,0:T(8,128)(2,1)}, u32[]{:S(2)}) copy-start(bf16[2,1536,192]{1,2,0:T(8,128)(2,1)} %param.25) | copy-start | bytes 3538948
  7.2 17.8 %copy-start.9 = (s32[2,32,8]{1,2,0:T(8,128)S(1)}, s32[2,32,8]{1,2,0:T(8,128)}, u32[]{:S(2)}) copy-start(s32[2,32,8]{1,2,0:T(8,128)} %param.19) | copy-start | bytes 6148
  10.2 18.1 %copy-start.8 = (bf16[2,1536]{1,0:T(2,128)(2,1)S(1)}, bf16[2,1536]{1,0:T(2,128)(2,1)}, u32[]{:S(2)}) copy-start(bf16[2,1536]{1,0:T(2,128)(2,1)} %param.29) | copy-start | bytes 18436
  10.2 18.1 %copy-start.11 = (bf16[2,1536,64]{1,2,0:T(8,128)(2,1)S(1)}, bf16[2,1536,64]{1,2,0:T(8,128)(2,1)}, u32[]{:S(2)}) copy-start(bf16[2,1536,64]{1,2,0:T(8,128)(2,1)} %param.27) | copy-start | bytes 1179652
  10.2 18.4 %all-to-all-start.1 = ((bf16[8,2,16384]{2,1,0:T(2,128)(2,1)}), bf16[8,2,16384]{2,1,0:T(2,128)(2,1)S(1)}, u32[]{:S(2)}, u32[]{:S(2)}) async-start(bf16[8,2,16384]{2,1,0:T(2,128)(2,1)} %reshape.468), calls=%async_computation.1 | async-start | bytes 1048576 | tf_op jit(solution)/shard_map/all_to_all | solution.py:69
  28.6 14.0 %all-to-all-start = ((bf16[8,2,16384]{2,1,0:T(2,128)(2,1)}), bf16[8,2,16384]{2,1,0:T(2,128)(2,1)S(1)}, u32[]{:S(2)}, u32[]{:S(2)}) async-start(bf16[8,2,16384]{2,1,0:T(2,128)(2,1)} %reshape.470), calls=%async_computation | async-start | bytes 1048576 | tf_op jit(solution)/shard_map/all_to_all | solution.py:69
  42.5 14.6 %all-to-all-start.3 = ((bf16[8,2,16384]{2,1,0:T(2,128)(2,1)}), bf16[8,2,16384]{2,1,0:T(2,128)(2,1)}, u32[]{:S(2)}, u32[]{:S(2)}) async-start(bf16[8,2,16384]{2,1,0:T(2,128)(2,1)} %reshape.466), calls=%async_computation.3 | async-start | bytes 1048576 | tf_op jit(solution)/shard_map/all_to_all | solution.py:69
  50.1 14.1 %copy-start = (bf16[32,8,16,1,64]{4,2,1,0,3:T(8,128)(2,1)}, bf16[32,8,16,1,64]{4,2,1,0,3:T(8,128)(2,1)S(1)}, u32[]{:S(2)}) copy-start(bf16[32,8,16,1,64]{4,2,1,0,3:T(8,128)(2,1)S(1)} %copy.109) | copy-start | bytes 1572868
  57.1 14.4 %all-to-all-start.2 = ((bf16[8,2,16384]{2,1,0:T(2,128)(2,1)}), bf16[8,2,16384]{2,1,0:T(2,128)(2,1)}, u32[]{:S(2)}, u32[]{:S(2)}) async-start(bf16[8,2,16384]{2,1,0:T(2,128)(2,1)} %reshape.472), calls=%async_computation.2 | async-start | bytes 1048576 | tf_op jit(solution)/shard_map/all_to_all | solution.py:69
  62.2 57.8 %all-reduce.5.cloned.1.call-start = ((), (), s32[]{:S(2)}) async-start(), calls=%async_computation.4 | async-start | bytes 196608 | tf_op jit(solution)/shard_map/psum | solution.py:56
  64.2 129.3 %all-reduce.7.cloned.1.call-start = ((), (), s32[]{:S(2)}) async-start(), calls=%async_computation.5 | async-start | bytes 196608 | tf_op jit(solution)/shard_map/psum | solution.py:58
  131.5 62.0 %copy-start.6 = (bf16[32,1536]{1,0:T(8,128)(2,1)S(1)}, bf16[32,1536]{1,0:T(8,128)(2,1)}, u32[]{:S(2)}) copy-start(bf16[32,1536]{1,0:T(8,128)(2,1)} %all-reduce.5.cloned.1.call-done) | copy-start | bytes 294916
  140.9 114.8 %all-reduce.9.cloned.1.call-start = ((), (), s32[]{:S(2)}) async-start(), calls=%async_computation.6 | async-start | bytes 196608 | tf_op jit(solution)/shard_map/psum | solution.py:56
  141.7 123.8 %copy-start.2 = (bf16[32,8,16,1,64]{4,2,1,0,3:T(8,128)(2,1)}, bf16[32,8,16,1,64]{4,2,1,0,3:T(8,128)(2,1)S(1)}, u32[]{:S(2)}) copy-start(bf16[32,8,16,1,64]{4,2,1,0,3:T(8,128)(2,1)S(1)} %copy.117) | copy-start | bytes 1572868
  203.1 126.2 %all-reduce.11.cloned.1.call-start = ((), (), s32[]{:S(2)}) async-start(), calls=%async_computation.7 | async-start | bytes 196608 | tf_op jit(solution)/shard_map/psum | solution.py:58
  267.3 9.4 %copy-start.1 = (bf16[32,8,16,1,64]{4,2,1,0,3:T(8,128)(2,1)S(1)}, bf16[32,8,16,1,64]{4,2,1,0,3:T(8,128)(2,1)}, u32[]{:S(2)}) copy-start(bf16[32,8,16,1,64]{4,2,1,0,3:T(8,128)(2,1)} %copy-done) | copy-start | bytes 1572868
  276.6 52.7 %copy-start.5 = (bf16[32,1536]{1,0:T(8,128)(2,1)S(1)}, bf16[32,1536]{1,0:T(8,128)(2,1)}, u32[]{:S(2)}) copy-start(bf16[32,1536]{1,0:T(8,128)(2,1)} %all-reduce.9.cloned.1.call-done) | copy-start | bytes 294916
Sparse Core Ops, SparseCore 0:
  65.9 54.0 all-reduce.4
  141.0 52.4 all-reduce.6
  203.2 52.4 all-reduce.8
  276.8 52.4 all-reduce.10
where the time goes:
time: 339 us; the launch traced here: 337 us
  waiting for transfers between devices  207 us (61%)
  matrix products  49.6 us (15%)
  local copies, waits for them, and re-layouts  30.4 us (9%)
  starting transfers between devices  21.9 us (6%)
  other arithmetic  14.5 us (4%)
  between operations  14.2 us (4%)
    psum x2, waiting for transfers between devices, decode_layer(): lax.psum(jnp.dot(attn_vec, w_o, preferred_element_type=jnp.float32).astyp...  98.4 us
    psum x2, waiting for transfers between devices, decode_layer(): lax.psum(expert_block(x_mid, choice, g_mlp, w_router, w_gate, w_up, w_dow...  89.9 us
    unnamed x40, local copies, waits for them, and re-layouts  26.9 us
    all_to_all x4, starting transfers between devices, local_step(): lax.all_to_all(cache_blk, 'tp', 2, 1, tiled=True)  21.3 us
    dot_general x2, matrix products, expert_block(): jnp.einsum('bef,efd->bd', expert_in, w_down, preferred_element_type=jnp.f...  18.6 us
    all_to_all x4, waiting for transfers between devices, local_step(): lax.all_to_all(cache_blk, 'tp', 2, 1, tiled=True)  18.3 us
    dot_general x2, matrix products, expert_block(): jnp.einsum('bd,edf->bef', normed, w_gate, preferred_element_type=jnp.floa...  15.5 us
  transfers between devices with their start and end apart: 8, of which 7 were waited for; matrix products, arithmetic and copies ran while one was open for 11% of the time, Pallas kernels for 0%

commit v1 on v0

v1 whole, which is shorter than its diff:
```python
import math

import jax
import jax.numpy as jnp
from jax import lax
from jax.experimental import pallas as pl
from jax.experimental.pallas import tpu as pltpu
from jax.sharding import PartitionSpec as P

EPS = 1e-5
THETA = 1000000.0
F32 = jnp.float32
BF16 = jnp.bfloat16
MESH = pl.DeviceIdType.MESH
NT = (((1,), (1,)), ((), ()))
TN = (((0,), (0,)), ((), ()))
CHUNK = 256
VMEM_BYTES = 67043328


def dot_nt(a, b):
    return lax.dot_general(a, b, NT, preferred_element_type=F32)


def iota(shape, dim):
    return lax.broadcasted_iota(jnp.int32, shape, dim)


def rms(h, gain):
    hf = h.astype(F32)
    scale = lax.rsqrt(jnp.mean(hf * hf, axis=-1, keepdims=True) + EPS)
    return (hf * scale * gain.astype(F32)).astype(BF16)


def make_kernel(n, rows, dim, seq, heads, head, experts, ff, top):
    half = rows // 2
    slots = seq // n
    q_heads = heads
    hidden_rows = experts * ff
    chunks = hidden_rows // CHUNK
    cut_cols = dim // (n // 2)
    parts = 3 * experts

    def kernel(hidden, lens, choice, k1, v1, k2, v2, g_attn, wq, wk, wv, wo, g_mlp, wr, wg, wu, wd,
               h_out, o0, o1, o2, o3,
               raw, tmp, send, recv, out_t, wqkv_v, wo_v, wr_v, wg_v, wu_v, wd_v, hs, ga_v, gm_v, ch_v,
               qs, kn, vn, sc, lrow, cosv, sinv, spread, gs_v, act, part, rs,
               raw_sem, small_sem, proj_sem, wg_sem, wu_sem, wd_sem, send_sem, recv_sem,
               rs_send, rs_recv, ag_send, ag_recv, out_sem):
        me = lax.axis_index('tp')
        caches = (k1, v1, k2, v2)
        outs = (o0, o1, o2, o3)

        def peer_of(d):
            return lax.rem(me + d, n)

        def copies_small():
            return [pltpu.make_async_copy(hidden, hs.at[0], small_sem.at[0]),
                    pltpu.make_async_copy(g_attn, ga_v, small_sem.at[1]),
                    pltpu.make_async_copy(g_mlp, gm_v, small_sem.at[2]),
                    pltpu.make_async_copy(choice, ch_v, small_sem.at[3]),
                    pltpu.make_async_copy(wr, wr_v, small_sem.at[4])]

        qw, kw = q_heads * head, head

        def copies_proj(l):
            return [pltpu.make_async_copy(wq.at[l], wqkv_v.at[l, pl.ds(0, qw)], proj_sem.at[l, 0]),
                    pltpu.make_async_copy(wk.at[l], wqkv_v.at[l, pl.ds(qw, kw)], proj_sem.at[l, 1]),
                    pltpu.make_async_copy(wv.at[l], wqkv_v.at[l, pl.ds(qw + kw, kw)], proj_sem.at[l, 2]),
                    pltpu.make_async_copy(wv.at[l], wqkv_v.at[l, pl.ds(qw + 2 * kw, kw)], proj_sem.at[l, 3]),
                    pltpu.make_async_copy(wo.at[l], wo_v.at[l], proj_sem.at[l, 4])]

        def copy_chunk(src, dst, sem, l, c):
            at = pl.ds(pl.multiple_of(c * CHUNK, CHUNK), CHUNK)
            return pltpu.make_async_copy(src.at[l, at], dst.at[l, at], sem.at[l, c])

        barrier = pltpu.get_barrier_semaphore()
        for d in range(1, n):
            pl.semaphore_signal(barrier, inc=1, device_id={'tp': peer_of(d)}, device_id_type=MESH)
        for c in range(2):
            pltpu.make_async_copy(caches[c], raw.at[c], raw_sem.at[c]).start()
        for cp in copies_small():
            cp.start()
        for cp in copies_proj(0):
            cp.start()
        for c in range(2, 4):
            pltpu.make_async_copy(caches[c], raw.at[c], raw_sem.at[c]).start()

        def start_weights(l):
            def go(c, carry):
                copy_chunk(wg, wg_v, wg_sem, l, c).start()
                copy_chunk(wu, wu_v, wu_sem, l, c).start()
                return carry
            lax.fori_loop(0, chunks, go, 0)

            def go_down(c, carry):
                copy_chunk(wd, wd_v, wd_sem, l, c).start()
                return carry
            lax.fori_loop(0, chunks, go_down, 0)

        start_weights(0)
        for cp in copies_proj(1):
            cp.start()
        start_weights(1)

        def pack(c):
            pltpu.make_async_copy(caches[c], raw.at[c], raw_sem.at[c]).wait()

            def step(i, carry):
                for u in range(4):
                    b = i * 4 + u
                    tmp[u, :, 0:head] = raw[c, b].astype(F32).reshape(slots * n, head)
                    tmp[u, :, head:2 * head] = raw[c, b + half].astype(F32).reshape(slots * n, head)
                for u in range(4):
                    b = i * 4 + u
                    for h in range(n):
                        send[c, h, b] = tmp[u, pl.ds(h, slots, stride=n), :].astype(BF16)
                return carry
            lax.fori_loop(0, half // 4, step, 0)

        def exchange(c, d):
            peer = peer_of(d)
            return pltpu.make_async_remote_copy(
                src_ref=send.at[c, peer], dst_ref=recv.at[c, :, me], send_sem=send_sem.at[c, d],
                recv_sem=recv_sem.at[c, me], device_id={'tp': peer}, device_id_type=MESH)

        def landed(c, d):
            peer = peer_of(d)
            return pltpu.make_async_remote_copy(
                src_ref=send.at[c, peer], dst_ref=recv.at[c, :, peer], send_sem=send_sem.at[c, d],
                recv_sem=recv_sem.at[c, peer], device_id={'tp': peer}, device_id_type=MESH)

        def send_cache(c):
            for d in range(1, n):
                exchange(c, d).start()

            def own(b, carry):
                recv[c, b, me] = send[c, me, b]
                return carry
            lax.fori_loop(0, half, own, 0)

        def wait_cache(c):
            for d in range(1, n):
                landed(c, d).wait_recv()

        pack(0)
        pl.semaphore_wait(barrier, n - 1)
        send_cache(0)
        pack(1)
        send_cache(1)

        for cp in copies_small():
            cp.wait()

        lane_c = iota((rows, 2 * head), 1)
        row_c = iota((rows, 2 * head), 0)
        len_c = jnp.zeros((rows, 2 * head), jnp.int32)
        for b in range(rows):
            len_c = jnp.where(row_c == b, lens[b], len_c)
        freq = jnp.exp((lane_c & (head // 2 - 1)).astype(F32) * (-2.0 * math.log(THETA) / head))
        angle = len_c.astype(F32) * freq
        cosv[...] = jnp.cos(angle)
        sine = jnp.sin(angle)
        lower = (lane_c & (head - 1)) < head // 2
        sinv[...] = jnp.where(lower, -sine, sine)
        row8 = iota((8, seq), 0)
        for b in range(half):
            lrow[pl.ds(8 * b, 8), :] = jnp.where(row8 < 4, lens[b], lens[b + half])
        part_row = iota((128, CHUNK), 0)
        part_e = jnp.where(part_row >= 2 * experts, part_row - 2 * experts,
                           jnp.where(part_row >= experts, part_row - experts, part_row))
        part_e = jnp.where(part_row >= parts, -1, part_e)
        col_e = iota((128, CHUNK), 1) // ff
        for c in range(chunks):
            spread[c] = jnp.where(part_e == col_e + c * (CHUNK // ff), 1.0, 0.0).astype(BF16)
        qs[...] = jnp.zeros_like(qs)

        lane16 = iota((half, 2 * head), 1)
        left16 = lane16 < head

        def swap(x):
            return pltpu.roll(x, head, 1)

        def rope(x):
            partner = jnp.where(lower, pltpu.roll(x, 2 * head - head // 2, 1), pltpu.roll(x, head // 2, 1))
            return (x * cosv[...] + partner * sinv[...]).astype(BF16).astype(F32)

        def project(l):
            for cp in copies_proj(l):
                cp.wait()
            a = rms(hs[2 * l], ga_v[l:l + 1, :])
            qkv = dot_nt(a, wqkv_v[l])
            t0 = rope(qkv[:, 0:2 * head])
            t1 = rope(qkv[:, 2 * head:4 * head])
            t2 = qkv[:, 4 * head:6 * head].astype(BF16).astype(F32)
            s0, s1 = swap(t0), swap(t1)
            zero = jnp.zeros((half, 2 * head), F32)
            qs[pl.ds(0, half, stride=8), :] = jnp.where(left16, t0[0:half], zero)
            qs[pl.ds(1, half, stride=8), :] = jnp.where(left16, s0[0:half], zero)
            qs[pl.ds(2, half, stride=8), :] = jnp.where(left16, t1[0:half], zero)
            qs[pl.ds(4, half, stride=8), :] = jnp.where(left16, zero, s0[half:rows])
            qs[pl.ds(5, half, stride=8), :] = jnp.where(left16, zero, t0[half:rows])
            qs[pl.ds(6, half, stride=8), :] = jnp.where(left16, zero, s1[half:rows])
            kn[...] = jnp.where(left16, s1[0:half], t1[half:rows])
            vn[...] = jnp.where(left16, t2[0:half], t2[half:rows])

        pos = iota((seq, 2 * head), 0)
        left_s = iota((seq, 2 * head), 1) < head

        def insert(c, b, new):
            at = jnp.where(left_s, lens[b], lens[b + half])
            x = recv[c, b].astype(F32).reshape(seq, 2 * head)
            x = jnp.where(pos == at, new[pl.ds(b, 1), :], x).astype(BF16)
            recv[c, b] = x.reshape(n, slots, 2 * head)
            return x

        def attend(l):
            kc, vc = 2 * l, 2 * l + 1
            wait_cache(kc)

            def k_step(i, carry):
                for u in range(4):
                    b = i * 4 + u
                    x = insert(kc, b, kn)
                    at = pl.ds(pl.multiple_of(b * 8, 8), 8)
                    sc[at, :] = dot_nt(qs[at, :].astype(BF16), x)
                return carry
            lax.fori_loop(0, half // 4, k_step, 0)
            s = sc[...] * head ** -0.5
            valid = iota((8 * half, seq), 1) <= lrow[...]
            s = jnp.where(valid, s, -1e30)
            e = jnp.exp(s - jnp.max(s, axis=-1, keepdims=True))
            sc[...] = e / jnp.sum(e, axis=-1, keepdims=True)
            wait_cache(vc)

            def v_step(i, carry):
                for u in range(4):
                    b = i * 4 + u
                    x = insert(vc, b, vn)
                    at = pl.ds(pl.multiple_of(b * 8, 8), 8)
                    sc[at, :] = jnp.dot(sc[at, :].astype(BF16), x, preferred_element_type=F32)
                return carry
            lax.fori_loop(0, half // 4, v_step, 0)
            up = [sc[pl.ds(j, half, stride=8), :] for j in range(3)]
            dn = [sc[pl.ds(4 + j, half, stride=8), :] for j in range(3)]
            t0 = jnp.concatenate([jnp.where(left16, up[0], swap(up[1])), jnp.where(left16, swap(dn[0]), dn[1])], axis=0)
            t1 = jnp.concatenate([up[2], swap(dn[2])], axis=0)
            t0 = t0.astype(BF16)
            t1 = t1[:, 0:head].astype(BF16)
            return (jnp.dot(t0, wo_v[l, 0:2 * head, :], preferred_element_type=F32)
                    + jnp.dot(t1, wo_v[l, 2 * head:3 * head, :], preferred_element_type=F32))

        def piece(p):
            return (pl.ds(pl.multiple_of((p // (n // 2)) * half, half), half),
                    pl.ds(pl.multiple_of((p % (n // 2)) * cut_cols, 128), cut_cols))

        def rs_copy(ar, d, src_slot):
            peer = peer_of(d)
            r, c = piece(peer)
            return pltpu.make_async_remote_copy(
                src_ref=part.at[ar, r, c], dst_ref=rs.at[ar, src_slot], send_sem=rs_send.at[ar, d],
                recv_sem=rs_recv.at[ar, src_slot], device_id={'tp': peer}, device_id_type=MESH)

        def ag_copy(ar, d, owner):
            peer = peer_of(d)
            r, c = piece(owner)
            return pltpu.make_async_remote_copy(
                src_ref=hs.at[ar + 1, r, c], dst_ref=hs.at[ar + 1, r, c], send_sem=ag_send.at[ar, d],
                recv_sem=ag_recv.at[ar, owner], device_id={'tp': peer}, device_id_type=MESH)

        def reduce_start(ar):
            for d in range(1, n):
                rs_copy(ar, d, me).start()

        def reduce_finish(ar):
            r, c = piece(me)
            acc = part[ar, r, c].astype(F32)
            for d in range(1, n):
                rs_copy(ar, d, peer_of(d)).wait_recv()
                acc = acc + rs[ar, peer_of(d)].astype(F32)
            hs[ar + 1, r, c] = (hs[ar, r, c].astype(F32) + acc).astype(BF16)
            for d in range(1, n):
                ag_copy(ar, d, me).start()

        def gather_finish(ar):
            for d in range(1, n):
                ag_copy(ar, d, peer_of(d)).wait_recv()

        def transpose_out(c):
            def step(i, carry):
                for u in range(2):
                    b = i * 2 + u
                    x = recv[c, b].astype(F32).reshape(seq, 2 * head).T.astype(BF16)
                    out_t[c, b] = x[0:head]
                    out_t[c, b + half] = x[head:2 * head]
                return carry
            lax.fori_loop(0, half // 2, step, 0)
            pltpu.make_async_copy(out_t.at[c], outs[c], out_sem.at[c]).start()

        def experts_of(l):
            m = rms(hs[2 * l + 1], gm_v[l:l + 1, :])
            logits = dot_nt(wr_v[l], m)
            row_e = iota((experts, rows), 0)
            picked = row_e == ch_v[l, 0:1, :]
            for t in range(1, top):
                picked = jnp.logical_or(picked, row_e == ch_v[l, t:t + 1, :])
            lg = jnp.where(picked, logits, -1e30)
            e = jnp.where(picked, jnp.exp(lg - jnp.max(lg, axis=0, keepdims=True)), 0.0)
            gate = e / jnp.sum(e, axis=0, keepdims=True)
            hi = gate.astype(BF16).astype(F32)
            mid = (gate - hi).astype(BF16).astype(F32)
            lo = (gate - hi - mid).astype(BF16).astype(F32)
            pad = jnp.zeros((128 - parts, rows), F32)
            gs_v[...] = jnp.concatenate([hi, mid, lo, pad], axis=0)
            gst = gs_v[...].astype(BF16)

            def up_step(c, carry):
                at = pl.ds(pl.multiple_of(c * CHUNK, CHUNK), CHUNK)
                copy_chunk(wg, wg_v, wg_sem, l, c).wait()
                copy_chunk(wu, wu_v, wu_sem, l, c).wait()
                g = dot_nt(m, wg_v[l, at, :])
                u = dot_nt(m, wu_v[l, at, :])
                w = lax.dot_general(gst, spread[c], TN, preferred_element_type=F32)
                act[c] = (g * jax.nn.sigmoid(g) * u * w).astype(BF16)
                return carry
            lax.fori_loop(0, chunks, up_step, 0)

            def wait_down(c, carry):
                copy_chunk(wd, wd_v, wd_sem, l, c).wait()
                return carry
            lax.fori_loop(0, chunks, wait_down, 0)
            u_all = jnp.concatenate([act[c] for c in range(chunks)], axis=1)

            def down_step(j, carry):
                at = pl.ds(pl.multiple_of(j * 256, 256), 256)
                y = jnp.dot(u_all, wd_v[l, :, at], preferred_element_type=F32)
                part[2 * l + 1, :, at] = y.astype(BF16)
                return carry
            lax.fori_loop(0, dim // 256, down_step, 0)

        for l in range(2):
            project(l)
            if l == 0:
                pack(2)
                send_cache(2)
            part[2 * l] = attend(l).astype(BF16)
            reduce_start(2 * l)
            if l == 0:
                pack(3)
                send_cache(3)
            reduce_finish(2 * l)
            transpose_out(2 * l)
            gather_finish(2 * l)
            experts_of(l)
            reduce_start(2 * l + 1)
            transpose_out(2 * l + 1)
            reduce_finish(2 * l + 1)
            gather_finish(2 * l + 1)

        final = pltpu.make_async_copy(hs.at[4], h_out, small_sem.at[0])
        final.start()
        for c in range(4):
            for d in range(1, n):
                exchange(c, d).wait_send()
        for ar in range(4):
            for d in range(1, n):
                rs_copy(ar, d, me).wait_send()
                ag_copy(ar, d, me).wait_send()
        for c in range(4):
            pltpu.make_async_copy(out_t.at[c], outs[c], out_sem.at[c]).wait()
        final.wait()

    return kernel


def solution(mesh):
    n = mesh.shape['tp']
    seq_spec = P('dp', 'tp', None, None)
    head_spec = P('dp', None, 'tp', None)
    col_spec = P(None, None, 'tp')
    ff_spec = P(None, None, None, 'tp')

    def local_step(hidden, lengths, choice, keys_one, vals_one, keys_two, vals_two, g_attn, w_q, w_k, w_v, w_o, g_mlp, w_router, w_gate, w_up, w_down):
        rows, dim = hidden.shape
        slots, head = keys_one.shape[1], keys_one.shape[3]
        seq = slots * n
        heads = w_q.shape[2] // head
        experts, ff = w_gate.shape[1], w_gate.shape[3]
        top = choice.shape[2]
        half = rows // 2
        hidden_rows = experts * ff
        chunks = hidden_rows // CHUNK
        cache_out = jax.ShapeDtypeStruct((rows, head, seq), BF16)
        dma = pltpu.SemaphoreType.DMA
        any_spec = pl.BlockSpec(memory_space=pl.ANY)
        smem_spec = pl.BlockSpec(memory_space=pltpu.SMEM)
        flip = lambda w: jnp.swapaxes(w, -1, -2)
        flat = lambda w: w.reshape(w.shape[0], hidden_rows, dim)
        outs = pl.pallas_call(
            make_kernel(n, rows, dim, seq, heads, head, experts, ff, top),
            out_shape=[jax.ShapeDtypeStruct((rows, dim), BF16)] + [cache_out] * 4,
            in_specs=[any_spec, smem_spec] + [any_spec] * 15,
            out_specs=[any_spec] * 5,
            scratch_shapes=[
                pltpu.VMEM((4, rows, slots, n, head), BF16),
                pltpu.VMEM((4, slots * n, 2 * head), F32),
                pltpu.VMEM((4, n, half, slots, 2 * head), BF16),
                pltpu.VMEM((4, half, n, slots, 2 * head), BF16),
                pltpu.VMEM((4, rows, head, seq), BF16),
                pltpu.VMEM((2, (heads + 3) * head, dim), BF16),
                pltpu.VMEM((2, heads * head, dim), BF16),
                pltpu.VMEM((2, experts, dim), BF16),
                pltpu.VMEM((2, hidden_rows, dim), BF16),
                pltpu.VMEM((2, hidden_rows, dim), BF16),
                pltpu.VMEM((2, hidden_rows, dim), BF16),
                pltpu.VMEM((5, rows, dim), BF16),
                pltpu.VMEM((2, dim), BF16),
                pltpu.VMEM((2, dim), BF16),
                pltpu.VMEM((2, top, rows), jnp.int32),
                pltpu.VMEM((8 * half, 2 * head), F32),
                pltpu.VMEM((half, 2 * head), F32),
                pltpu.VMEM((half, 2 * head), F32),
                pltpu.VMEM((8 * half, seq), F32),
                pltpu.VMEM((8 * half, seq), jnp.int32),
                pltpu.VMEM((rows, 2 * head), F32),
                pltpu.VMEM((rows, 2 * head), F32),
                pltpu.VMEM((chunks, 128, CHUNK), BF16),
                pltpu.VMEM((128, rows), F32),
                pltpu.VMEM((chunks, rows, CHUNK), BF16),
                pltpu.VMEM((4, rows, dim), BF16),
                pltpu.VMEM((4, n, half, dim // (n // 2)), BF16),
                dma((4,)), dma((5,)), dma((2, 5)), dma((2, chunks)), dma((2, chunks)), dma((2, chunks)),
                dma((4, n)), dma((4, n)), dma((4, n)), dma((4, n)), dma((4, n)), dma((4, n)), dma((4,)),
            ],
            compiler_params=pltpu.CompilerParams(
                collective_id=0, has_side_effects=True, vmem_limit_bytes=VMEM_BYTES),
            name='decode_two_layers',
        )(hidden, lengths, flip(choice), keys_one, vals_one, keys_two, vals_two, g_attn,
          flip(w_q), flip(w_k), flip(w_v), w_o, g_mlp, flip(w_router),
          flat(flip(w_gate)), flat(flip(w_up)), flat(w_down))
        back = lambda o: flip(o)[:, :, None, :]
        return (outs[0], back(outs[1]), back(outs[2]), back(outs[3]), back(outs[4]))

    return jax.shard_map(local_step, mesh=mesh, in_specs=(P('dp', None), P('dp'), P(None, 'dp', None), seq_spec, seq_spec, seq_spec, seq_spec, P(), col_spec, col_spec, col_spec, P(None, 'tp', None), P(), P(), ff_spec, ff_spec, P(None, None, 'tp', None)), out_specs=(P('dp', None), head_spec, head_spec, head_spec, head_spec), check_vma=False)
```

time: 339 us -> 87.4 us (0.26)
  waiting for transfers between devices: 207 us -> 0 us
  Pallas kernels: 0 us -> 77.5 us
  matrix products: 49.6 us -> 0 us
  starting transfers between devices: 21.9 us -> 0 us
  local copies, waits for them, and re-layouts: 30.4 us -> 9.01 us
  other arithmetic: 14.5 us -> 0 us
  between operations: 14.2 us -> 0.65 us
    psum x4 -> x0, waiting for transfers between devices: 188 us -> none  [the longest x2 98.4 us: decode_layer(): lax.psum(jnp.dot(attn_vec, w_o, preferred_element_type=jnp.float32).astyp...]
    pallas_call x0 -> x1, Pallas kernels: none -> 77.5 us  [local_step(): pl.pallas_call(make_kernel(n, rows, dim, seq, heads, head, experts, ff, t...]
    dot_general x18 -> x0, matrix products: 49.6 us -> none  [the longest x2 18.6 us: expert_block(): jnp.einsum('bef,efd->bd', expert_in, w_down, preferred_element_type=jnp.f...]
    all_to_all x4 -> x0, starting transfers between devices: 21.3 us -> none  [local_step(): lax.all_to_all(cache_blk, 'tp', 2, 1, tiled=True)]
    all_to_all x4 -> x0, waiting for transfers between devices: 18.3 us -> none  [local_step(): lax.all_to_all(cache_blk, 'tp', 2, 1, tiled=True)]
    unnamed x40 -> x5, local copies, waits for them, and re-layouts: 26.9 us -> 9.01 us
    select_n x1 -> x0, other arithmetic: 5.13 us -> none  [decode_layer(): val_cache = jnp.where(is_new, val_new[:, None], val_cache)]
    reduce_sum x10 -> x0, other arithmetic: 4 us -> none  [the longest x4 3.24 us: rms_norm(): jnp.mean(tensor_f * tensor_f, axis=-1, keepdims=True) + EPS]
  transfers between devices with their start and end apart: 8 -> 0, of which waited for: 7 -> 0; matrix products, arithmetic and copies ran while one was open for 11% -> 0% of each run, Pallas kernels for 0% -> 0%
where the time goes in v1:
time: 87.4 us; the launch traced here: 87.1 us
  Pallas kernels  77.5 us (89%)
  local copies, waits for them, and re-layouts  9.01 us (10%)
    pallas_call x1, Pallas kernels, local_step(): pl.pallas_call(make_kernel(n, rows, dim, seq, heads, head, experts, ff, t...  77.5 us
    unnamed x5, local copies, waits for them, and re-layouts  9.01 us

profile of v1, /device:TPU:81, one launch (start us, length us, event | category | flops | bytes accessed | tf_op | source)
XLA Modules:
  0.0 87.1 jit_solution(5618544157000473086)
XLA Ops:
  0.6 77.5 %decode_two_layers.1 = (bf16[32,1536]{1,0:T(8,128)(2,1)}, bf16[32,64,128]{2,1,0:T(8,128)(2,1)}, bf16[32,64,128]{2,1,0:T(8,128)(2,1)}, bf16[32,64,128]{2,1,0:T(8,128)(2,1)}, bf16[32,64,128]{2,1,0:T(8,128)(2,1)}) custom-call(bf16[32,1536]{1,0:T(8,128)(2,1)} %hidden.1, s32[32]{0:T(128)} %lens.1, s32[2,8,32]{2,1,0:T(8,128)} %bitcast.43, ...), custom_call_target="tpu_custom_call" | custom-call | tf_op jit(solution)/shard_map/decode_two_layers/pallas_call | solution.py:399
  78.1 1.5 %copy.31 = bf16[32,1536]{1,0:T(8,128)(2,1)} copy(bf16[32,1536]{1,0:T(8,128)(2,1)} %get-tuple-element.25) | data formatting | bytes 196608
  79.6 1.9 %copy.32 = bf16[32,128,1,64]{1,3,2,0:T(8,128)(2,1)} copy(bf16[32,128,1,64]{1,3,2,0:T(8,128)(2,1)} %bitcast.39) | data formatting | bytes 1048576
  81.5 1.9 %copy.33 = bf16[32,128,1,64]{1,3,2,0:T(8,128)(2,1)} copy(bf16[32,128,1,64]{1,3,2,0:T(8,128)(2,1)} %bitcast.38) | data formatting | bytes 1048576
  83.4 1.9 %copy.34 = bf16[32,128,1,64]{1,3,2,0:T(8,128)(2,1)} copy(bf16[32,128,1,64]{1,3,2,0:T(8,128)(2,1)} %bitcast.37) | data formatting | bytes 1048576
  85.2 1.9 %copy.35 = bf16[32,128,1,64]{1,3,2,0:T(8,128)(2,1)} copy(bf16[32,128,1,64]{1,3,2,0:T(8,128)(2,1)} %bitcast.36) | data formatting | bytes 1048576

commit v2 on v1

--- a/solution.py
+++ b/solution.py
@@ -15,6 +15,9 @@
 NT = (((1,), (1,)), ((), ()))
 TN = (((0,), (0,)), ((), ()))
 CHUNK = 256
+UP_UNROLL = 10
+DOWN_UNROLL = 6
+DOWN = 256
 VMEM_BYTES = 67043328
 
 
@@ -118,40 +121,51 @@
                 return carry
             lax.fori_loop(0, half // 4, step, 0)
 
-        def exchange(c, d):
+        quarter = half // 2
+
+        def exchange(c, d, k, owner):
             peer = peer_of(d)
+            at = pl.ds(k * quarter, quarter)
             return pltpu.make_async_remote_copy(
-                src_ref=send.at[c, peer], dst_ref=recv.at[c, :, me], send_sem=send_sem.at[c, d],
-                recv_sem=recv_sem.at[c, me], device_id={'tp': peer}, device_id_type=MESH)
-
-        def landed(c, d):
-            peer = peer_of(d)
-            return pltpu.make_async_remote_copy(
-                src_ref=send.at[c, peer], dst_ref=recv.at[c, :, peer], send_sem=send_sem.at[c, d],
-                recv_sem=recv_sem.at[c, peer], device_id={'tp': peer}, device_id_type=MESH)
-
-        def send_cache(c):
+                src_ref=send.at[c, peer, at], dst_ref=recv.at[c, at, owner], send_sem=send_sem.at[c, k, d],
+                recv_sem=recv_sem.at[c, k, owner], device_id={'tp': peer}, device_id_type=MESH)
+
+        def send_half(c, k):
             for d in range(1, n):
-                exchange(c, d).start()
-
+                exchange(c, d, k, me).start()
+
+        def keep_own(c):
             def own(b, carry):
                 recv[c, b, me] = send[c, me, b]
                 return carry
             lax.fori_loop(0, half, own, 0)
 
+        def send_cache(c):
+            send_half(c, 0)
+            send_half(c, 1)
+            keep_own(c)
+
         def wait_cache(c):
-            for d in range(1, n):
-                landed(c, d).wait_recv()
-
-        pack(0)
-        pl.semaphore_wait(barrier, n - 1)
-        send_cache(0)
-        pack(1)
-        send_cache(1)
+            for k in range(2):
+                for d in range(1, n):
+                    exchange(c, d, k, peer_of(d)).wait_recv()
+
+        with jax.named_scope('pack_0'):
+            pack(0)
+        with jax.named_scope('enter'):
+            pl.semaphore_wait(barrier, n - 1)
+        with jax.named_scope('send_0'):
+            send_cache(0)
+        with jax.named_scope('pack_1'):
+            pack(1)
+        with jax.named_scope('send_1'):
+            send_cache(1)
 
         for cp in copies_small():
             cp.wait()
 
+        tables = jax.named_scope('tables')
+        tables.__enter__()
         lane_c = iota((rows, 2 * head), 1)
         row_c = iota((rows, 2 * head), 0)
         len_c = jnp.zeros((rows, 2 * head), jnp.int32)
@@ -174,6 +188,7 @@
         for c in range(chunks):
             spread[c] = jnp.where(part_e == col_e + c * (CHUNK // ff), 1.0, 0.0).astype(BF16)
         qs[...] = jnp.zeros_like(qs)
+        tables.__exit__(None, None, None)
 
         lane16 = iota((half, 2 * head), 1)
         left16 = lane16 < head
@@ -216,7 +231,8 @@
 
         def attend(l):
             kc, vc = 2 * l, 2 * l + 1
-            wait_cache(kc)
+            with jax.named_scope(f'wait_k{l}'):
+                wait_cache(kc)
 
             def k_step(i, carry):
                 for u in range(4):
@@ -231,7 +247,8 @@
             s = jnp.where(valid, s, -1e30)
             e = jnp.exp(s - jnp.max(s, axis=-1, keepdims=True))
             sc[...] = e / jnp.sum(e, axis=-1, keepdims=True)
-            wait_cache(vc)
+            with jax.named_scope(f'wait_v{l}'):
+                wait_cache(vc)
 
             def v_step(i, carry):
                 for u in range(4):
@@ -298,6 +315,8 @@
             pltpu.make_async_copy(out_t.at[c], outs[c], out_sem.at[c]).start()
 
         def experts_of(l):
+            gate_scope = jax.named_scope(f'gate_{l}')
+            gate_scope.__enter__()
             m = rms(hs[2 * l + 1], gm_v[l:l + 1, :])
             logits = dot_nt(wr_v[l], m)
             row_e = iota((experts, rows), 0)
@@ -313,6 +332,7 @@
             pad = jnp.zeros((128 - parts, rows), F32)
             gs_v[...] = jnp.concatenate([hi, mid, lo, pad], axis=0)
             gst = gs_v[...].astype(BF16)
+            gate_scope.__exit__(None, None, None)
 
             def up_step(c, carry):
                 at = pl.ds(pl.multiple_of(c * CHUNK, CHUNK), CHUNK)
@@ -323,7 +343,8 @@
                 w = lax.dot_general(gst, spread[c], TN, preferred_element_type=F32)
                 act[c] = (g * jax.nn.sigmoid(g) * u * w).astype(BF16)
                 return carry
-            lax.fori_loop(0, chunks, up_step, 0)
+            with jax.named_scope(f'up_{l}'):
+                lax.fori_loop(0, chunks, up_step, 0, unroll=UP_UNROLL)
 
             def wait_down(c, carry):
                 copy_chunk(wd, wd_v, wd_sem, l, c).wait()
@@ -332,36 +353,57 @@
             u_all = jnp.concatenate([act[c] for c in range(chunks)], axis=1)
 
             def down_step(j, carry):
-                at = pl.ds(pl.multiple_of(j * 256, 256), 256)
+                at = pl.ds(pl.multiple_of(j * DOWN, DOWN), DOWN)
                 y = jnp.dot(u_all, wd_v[l, :, at], preferred_element_type=F32)
                 part[2 * l + 1, :, at] = y.astype(BF16)
                 return carry
-            lax.fori_loop(0, dim // 256, down_step, 0)
+            with jax.named_scope(f'down_{l}'):
+                lax.fori_loop(0, dim // DOWN, down_step, 0, unroll=DOWN_UNROLL)
 
         for l in range(2):
-            project(l)
+            with jax.named_scope(f'project_{l}'):
+                project(l)
+            with jax.named_scope(f'attend_{l}'):
+                part[2 * l] = attend(l).astype(BF16)
+            with jax.named_scope(f'rs_a{l}'):
+                reduce_start(2 * l)
             if l == 0:
-                pack(2)
-                send_cache(2)
-            part[2 * l] = attend(l).astype(BF16)
-            reduce_start(2 * l)
+                with jax.named_scope('pack_2'):
+                    pack(2)
+                    send_half(2, 0)
+            with jax.named_scope(f'rs_a{l}_fin'):
+                reduce_finish(2 * l)
             if l == 0:
-                pack(3)
-                send_cache(3)
-            reduce_finish(2 * l)
-            transpose_out(2 * l)
-            gather_finish(2 * l)
+                with jax.named_scope('pack_3'):
+                    send_half(2, 1)
+                    keep_own(2)
+                    pack(3)
+            with jax.named_scope(f'tr_a{l}'):
+                transpose_out(2 * l)
+            with jax.named_scope(f'ag_a{l}'):
+                gather_finish(2 * l)
+            if l == 0:
+                send_half(3, 0)
+                send_half(3, 1)
+                keep_own(3)
             experts_of(l)
-            reduce_start(2 * l + 1)
-            transpose_out(2 * l + 1)
-            reduce_finish(2 * l + 1)
-            gather_finish(2 * l + 1)
+            with jax.named_scope(f'rs_m{l}'):
+                reduce_start(2 * l + 1)
+            with jax.named_scope(f'tr_m{l}'):
+                transpose_out(2 * l + 1)
+            with jax.named_scope(f'rs_m{l}_fin'):
+                reduce_finish(2 * l + 1)
+            with jax.named_scope(f'ag_m{l}'):
+                gather_finish(2 * l + 1)
 
         final = pltpu.make_async_copy(hs.at[4], h_out, small_sem.at[0])
         final.start()
+        tail = jax.named_scope('tail')
+        tail.__enter__()
         for c in range(4):
-            for d in range(1, n):
-                exchange(c, d).wait_send()
+            for k in range(2):
+                for d in range(1, n):
+                    exchange(c, d, k, me).wait_send()
         for ar in range(4):
             for d in range(1, n):
                 rs_copy(ar, d, me).wait_send()
@@ -369,8 +411,28 @@
         for c in range(4):
             pltpu.make_async_copy(out_t.at[c], outs[c], out_sem.at[c]).wait()
         final.wait()
+        tail.__exit__(None, None, None)
 
     return kernel
+
+
+def pass_on(*refs):
+    src, dst, mid, in_sem, out_sem = refs[0:5], refs[5:10], refs[10:15], refs[15], refs[16]
+
+    def part(ref, k):
+        size = ref.shape[0] // 2
+        return ref.at[pl.ds(k * size, size)]
+
+    moves = [(i, k) for i in range(5) for k in range(2)]
+    into = [pltpu.make_async_copy(part(src[i], k), part(mid[i], k), in_sem.at[i, k]) for i, k in moves]
+    away = [pltpu.make_async_copy(part(mid[i], k), part(dst[i], k), out_sem.at[i, k]) for i, k in moves]
+    for cp in into:
+        cp.start()
+    for a, b in zip(into, away):
+        a.wait()
+        b.start()
+    for cp in away:
+        cp.wait()
 
 
 def solution(mesh):
@@ -430,7 +492,7 @@
                 pltpu.VMEM((4, rows, dim), BF16),
                 pltpu.VMEM((4, n, half, dim // (n // 2)), BF16),
                 dma((4,)), dma((5,)), dma((2, 5)), dma((2, chunks)), dma((2, chunks)), dma((2, chunks)),
-                dma((4, n)), dma((4, n)), dma((4, n)), dma((4, n)), dma((4, n)), dma((4, n)), dma((4,)),
+                dma((4, 2, n)), dma((4, 2, n)), dma((4, n)), dma((4, n)), dma((4, n)), dma((4, n)), dma((4,)),
             ],
             compiler_params=pltpu.CompilerParams(
                 collective_id=0, has_side_effects=True, vmem_limit_bytes=VMEM_BYTES),
@@ -438,6 +500,14 @@
         )(hidden, lengths, flip(choice), keys_one, vals_one, keys_two, vals_two, g_attn,
           flip(w_q), flip(w_k), flip(w_v), w_o, g_mlp, flip(w_router),
           flat(flip(w_gate)), flat(flip(w_up)), flat(w_down))
+        outs = pl.pallas_call(
+            pass_on,
+            out_shape=[jax.ShapeDtypeStruct(o.shape, o.dtype) for o in outs],
+            in_specs=[any_spec] * 5,
+            out_specs=[any_spec] * 5,
+            scratch_shapes=[pltpu.VMEM(o.shape, o.dtype) for o in outs] + [dma((5, 2)), dma((5, 2))],
+            name='pass_on',
+        )(*outs)
         back = lambda o: flip(o)[:, :, None, :]
         return (outs[0], back(outs[1]), back(outs[2]), back(outs[3]), back(outs[4]))
 

time: 87.4 us -> 76.3 us (0.87)
  local copies, waits for them, and re-layouts: 9.01 us -> 0 us
  Pallas kernels: 77.5 us -> 75.6 us
    unnamed x5 -> x0, local copies, waits for them, and re-layouts: 9.01 us -> none
    pallas_call x1, Pallas kernels: 77.5 us -> 73.1 us  [local_step(): pl.pallas_call(make_kernel(n, rows, dim, seq, heads, head, experts, ff, t...]
    pallas_call x0 -> x1, Pallas kernels: none -> 2.49 us  [local_step(): pl.pallas_call(pass_on, out_shape=[jax.ShapeDtypeStruct(o.shape, o.dtype)...]
where the time goes in v2:
time: 76.3 us; the launch traced here: 76.2 us
  Pallas kernels  75.6 us (99%)
    pallas_call x1, Pallas kernels, local_step(): pl.pallas_call(make_kernel(n, rows, dim, seq, heads, head, experts, ff, t...  73.1 us
    pallas_call x1, Pallas kernels, local_step(): pl.pallas_call(pass_on, out_shape=[jax.ShapeDtypeStruct(o.shape, o.dtype)...  2.49 us

profile of v2, /device:TPU:81, one launch (start us, length us, event | category | flops | bytes accessed | tf_op | source)
XLA Modules:
  0.0 76.2 jit_solution(4962521928615370038)
XLA Ops:
  0.6 73.1 %decode_two_layers.1 = (bf16[32,1536]{1,0:T(8,128)(2,1)}, bf16[32,64,128]{2,1,0:T(8,128)(2,1)}, bf16[32,64,128]{2,1,0:T(8,128)(2,1)}, bf16[32,64,128]{2,1,0:T(8,128)(2,1)}, bf16[32,64,128]{2,1,0:T(8,128)(2,1)}) custom-call(bf16[32,1536]{1,0:T(8,128)(2,1)} %hidden.1, s32[32]{0:T(128)} %lens.1, s32[2,8,32]{2,1,0:T(8,128)} %bitcast.39, ...), custom_call_target="tpu_custom_call" | custom-call | tf_op jit(solution)/shard_map/decode_two_layers/pallas_call | solution.py:461
  73.7 2.5 %pass_on.1 = (bf16[32,1536]{1,0:T(8,128)(2,1)}, bf16[32,64,128]{2,1,0:T(8,128)(2,1)}, bf16[32,64,128]{2,1,0:T(8,128)(2,1)}, bf16[32,64,128]{2,1,0:T(8,128)(2,1)}, bf16[32,64,128]{2,1,0:T(8,128)(2,1)}) custom-call(bf16[32,1536]{1,0:T(8,128)(2,1)} %get-tuple-element.15.refs_0_, bf16[32,64,128]{2,1,0:T(8,128)(2,1)} %get-tuple-element.16.refs_1_, ...), custom_call_target="tpu_custom_call" | custom-call | tf_op jit(solution)/shard_map/pass_on/pallas_call | solution.py:503
